TPU v7x, 32 devices: a whole 2x2x4 slice. The times are simulated.
32 devices in a mesh: section: 4 (over y, x), ctx: 4 (over z), dp: 2 (over core).
Axes of the slice: x: 2, y: 2, z: 4, core: 2. Of those that a mesh axis runs over, the one named last changes fastest.
Arguments:
- first_input: bfloat16 [4, 2, 512, 2048], P('section', 'dp', 'ctx'), may hold values from -14 to 14
- second_input: bfloat16 [4, 2, 512, 2048], P('section', 'dp', 'ctx'), may hold values from -6 to 6
- upstream: bfloat16 [4, 2, 512, 2048], P('section', 'dp', 'ctx'), may hold values from -6 to 6
- first_picks: int32 [4, 2, 512, 6], P('section', 'dp', 'ctx'), may hold values from 0 to 63, all different within a row
- second_picks: int32 [4, 2, 512, 6], P('section', 'dp', 'ctx'), may hold values from 0 to 63, all different within a row
- gate_grads: float32 [4, 2, 512, 6], P('section', 'dp', 'ctx'), may hold values from -0.0009 to 0.0009
- norm_gain: float32 [4, 2048], P('section'), may hold values from 0.5 to 1.5
- router_weight: float32 [4, 64, 2048], P('section'), may hold values from -0.25 to 0.25
- gate_weight: bfloat16 [4, 2048, 1280], P('section', 'ctx'), may hold values from -0.125 to 0.125
- up_weight: bfloat16 [4, 2048, 1280], P('section', 'ctx'), may hold values from -0.125 to 0.125
- down_weight: bfloat16 [4, 1280, 2048], P('section', None, 'ctx'), may hold values from -0.15625 to 0.15625
Outputs:
- arrived: bfloat16 [4, 2, 512, 2048], P('section', 'dp', 'ctx')
- routing: float32 [4, 2, 512, 6], P('section', 'dp', 'ctx')
- input_grad: bfloat16 [4, 2, 512, 2048], P('section', 'dp', 'ctx')
- router_grad: float32 [4, 64, 2048], P('section')
- balance: float32 [4, 2, 2], P('section', 'dp')
Inputs may be any that keep to these rules, and one draw needn't show every extreme that they name: `first_picks`: each token names 6 different experts. `second_picks`: each token names 6 different experts.
All inputs are finite; a program needn't handle non-finite values.
Results may differ from a plain program's by a relative error of at most 0.002.
The roundings to bfloat16 on the way count: a program that leaves them out, or rounds other values in their place, can miss the bound.
Values may be sent and summed in bfloat16 or wider, within the bound.
No kernel may reach another device: no remote copies, remote signals or barrier semaphores. Data moves between devices by JAX's collectives and lax.ppermute only.
A program may use at most 64 MiB of HBM per device.

v0:
```python
import jax
import jax.numpy as jnp
from jax import lax
from jax.sharding import PartitionSpec as P

EPSILON = 1e-06
ROUTE_SCALE = 2.5


def shifted(block, axis, distance):
    devices = range(lax.axis_size(axis))
    route = [((i - distance) % len(devices), i) for i in devices]
    return lax.ppermute(block, axis, route)


def normalize(values_in, norm_gain):
    values = values_in.astype(jnp.float32)
    inverse = lax.rsqrt(jnp.mean(values * values, axis=-1, keepdims=True) + EPSILON)
    return ((values * inverse * norm_gain).astype(jnp.bfloat16), inverse)


def one_hot(picks, experts):
    labels = jnp.arange(experts, dtype=jnp.int32)
    return (picks[:, :, None] == labels[None, None, :]).astype(jnp.float32)


def scores(normed, router_w, table):
    logits = jnp.dot(normed.astype(jnp.float32), router_w.T, precision=lax.Precision.HIGHEST)
    affinity = jax.nn.sigmoid(logits)
    chosen = jnp.einsum("tke,te->tk", table, affinity, precision=lax.Precision.HIGHEST)
    chosen_sum = jnp.sum(chosen, axis=-1, keepdims=True)
    gate_weights = ROUTE_SCALE * chosen / chosen_sum
    spread = jnp.sum(affinity, axis=-1, keepdims=True)
    shares = affinity / spread
    return (affinity, chosen, chosen_sum, gate_weights, spread, shares)


def router_back(grads, table, affinity, chosen, chosen_sum, spread, shares, frac, length):
    chosen_grad = ROUTE_SCALE * (
        grads / chosen_sum
        - jnp.sum(grads * chosen, axis=-1, keepdims=True) / (chosen_sum * chosen_sum)
    )
    affinity_grad = jnp.einsum("tk,tke->te", chosen_grad, table, precision=lax.Precision.HIGHEST)
    share_grad = frac[None, :] / length
    affinity_grad = (
        affinity_grad + (share_grad - jnp.sum(share_grad * shares, axis=-1, keepdims=True)) / spread
    )
    return affinity_grad * affinity * (1.0 - affinity)


def shared_back(hidden_grad, gate_pre, up_pre):
    sigmoid_v = jax.nn.sigmoid(gate_pre)
    slope = sigmoid_v * (1.0 + gate_pre * (1.0 - sigmoid_v))
    gate_grad = (hidden_grad * up_pre * slope).astype(jnp.bfloat16)
    up_grad = (hidden_grad * gate_pre * sigmoid_v).astype(jnp.bfloat16)
    return (gate_grad, up_grad)


def norm_back(values_in, inverse, norm_gain, normed_grad):
    values = values_in.astype(jnp.float32)
    scaled = normed_grad * norm_gain
    return inverse * (
        scaled - values * inverse * inverse * jnp.mean(scaled * values, axis=-1, keepdims=True)
    )


def shards(
    first_input,
    second_input,
    upstream,
    first_picks,
    second_picks,
    gate_grads,
    norm_gain,
    router_weight,
    gate_weight,
    up_weight,
    down_weight,
):
    first_in = first_input[0, 0]
    second_in = second_input[0, 0]
    first_pk = first_picks[0, 0]
    second_pk = second_picks[0, 0]
    grads = gate_grads[0, 0]
    gain_s = norm_gain[0]
    router_w = router_weight[0]
    experts = router_w.shape[0]
    tokens = first_in.shape[0]
    per_token = first_pk.shape[1]
    length = tokens * lax.axis_size("ctx")
    table_a = one_hot(first_pk, experts)
    table_b = one_hot(second_pk, experts)
    counts_a = jnp.sum(table_a, axis=(0, 1))
    counts_b = jnp.sum(table_b, axis=(0, 1))
    returned = shifted(upstream[0, 0], "section", -1)
    normed_a, inverse_a = normalize(first_in, gain_s)
    normed_b, inverse_b = normalize(second_in, gain_s)
    aff_a, chosen_a, csum_a, routing_a, spread_a, shares_a = scores(normed_a, router_w, table_a)
    aff_b, chosen_b, csum_b, routing_b, spread_b, shares_b = scores(normed_b, router_w, table_b)
    sums_a = jnp.sum(shares_a, axis=0)
    sums_b = jnp.sum(shares_b, axis=0)
    counts_a, counts_b, sums_a, sums_b = lax.psum((counts_a, counts_b, sums_a, sums_b), "ctx")
    frac_a = experts / (per_token * length) * counts_a
    frac_b = experts / (per_token * length) * counts_b
    balance = jnp.stack([jnp.sum(frac_a * sums_a / length), jnp.sum(frac_b * sums_b / length)])
    stacked = jnp.concatenate([normed_a, normed_b], axis=0)
    gate_full, up_full, down_full = (
        lax.all_gather(gate_weight[0], "ctx", axis=0, tiled=True),
        lax.all_gather(up_weight[0], "ctx", axis=0, tiled=True),
        lax.all_gather(down_weight[0], "ctx", axis=1, tiled=True),
    )
    gate_pre = jnp.dot(stacked, gate_full, preferred_element_type=jnp.float32)
    up_pre = jnp.dot(stacked, up_full, preferred_element_type=jnp.float32)
    hidden = (jax.nn.silu(gate_pre) * up_pre).astype(jnp.bfloat16)
    projected = jnp.dot(hidden[:tokens], down_full, preferred_element_type=jnp.float32)
    hidden_grad = jnp.einsum("td,fd->tf", returned, down_full, preferred_element_type=jnp.float32)
    output_a = (first_in.astype(jnp.float32) + projected).astype(jnp.bfloat16)
    arrived = shifted(output_a, "section", 1)
    gate_grad, up_grad = shared_back(hidden_grad, gate_pre[tokens:], up_pre[tokens:])
    normed_grad = jnp.einsum("tf,df->td", gate_grad, gate_full, preferred_element_type=jnp.float32)
    normed_grad = normed_grad + jnp.einsum(
        "tf,df->td", up_grad, up_full, preferred_element_type=jnp.float32
    )
    logit_grad = router_back(
        grads, table_b, aff_b, chosen_b, csum_b, spread_b, shares_b, frac_b, length
    )
    router_part = jnp.dot(
        logit_grad.T, normed_b.astype(jnp.float32), precision=lax.Precision.HIGHEST
    )
    normed_grad = normed_grad + jnp.dot(logit_grad, router_w, precision=lax.Precision.HIGHEST)
    input_grad = (
        returned.astype(jnp.float32) + norm_back(second_in, inverse_b, gain_s, normed_grad)
    ).astype(jnp.bfloat16)
    router_total = lax.psum(router_part, ("ctx", "dp"))
    return (
        arrived[None, None],
        routing_a[None, None],
        input_grad[None, None],
        router_total[None],
        balance[None, None],
    )


def solution(mesh):
    in_specs = (
        P("section", "dp", "ctx", None),
        P("section", "dp", "ctx", None),
        P("section", "dp", "ctx", None),
        P("section", "dp", "ctx", None),
        P("section", "dp", "ctx", None),
        P("section", "dp", "ctx", None),
        P("section", None),
        P("section", None, None),
        P("section", "ctx", None),
        P("section", "ctx", None),
        P("section", None, "ctx"),
    )
    out_specs = (
        P("section", "dp", "ctx", None),
        P("section", "dp", "ctx", None),
        P("section", "dp", "ctx", None),
        P("section", None, None),
        P("section", "dp", None),
    )
    return jax.shard_map(shards, mesh=mesh, in_specs=in_specs, out_specs=out_specs, check_vma=False)
```

profile of v0, /device:TPU:0, one launch (start us, length us, event | category | flops | bytes accessed | tf_op | source)
XLA Modules:
  0.0 339.5 jit_solution(7812694570531143835)
XLA Ops:
  8.0 0.0 copy-start
  8.0 0.0 copy-start.8
  8.0 0.0 copy-start.1
  8.0 0.0 copy-start.6
  8.0 0.0 all-gather.9.cloned.1.call-start
  8.1 0.7 all-gather.9.cloned.1.call-update
  8.8 0.0 copy-start.7
  8.8 0.0 copy-start.3
  8.8 0.0 all-gather.7.cloned.1.call-start
  8.8 0.7 all-gather.7.cloned.1.call-update
  9.5 0.0 all-gather.11.cloned.1.call-start
  9.6 0.7 all-gather.11.cloned.1.call-update
  10.3 0.0 all-reduce.3.cloned.1.call-start
  10.3 4.0 %collective-permute-start.1 = (bf16[128,2048]{1,0:T(8,128)(2,1)}, bf16[128,2048]{1,0:T(8,128)(2,1)S(1)}, u32[]{:S(2)}, u32[]{:S(2)}) collective-permute-start(bf16[128,2048]{1,0:T(8,128)(2,1)} %bitcast.11), channel_id=1, source_target_pairs={{8,0},{16,8},{24,16},{0,24},{9,1},{17,9},{25,17},{1,25},{10,2},{18... | collective-permute-start | bytes 1572872 | tf_op jit(solution)/shard_map/ppermute | solution.py:13
  14.3 0.0 copy-done.8
  14.3 0.0 copy-done.1
  14.3 0.2 fusion.44
  14.5 0.0 copy-done
  14.5 0.0 copy-done.6
  14.5 0.8 fusion.84
  15.3 0.0 copy-done.7
  15.4 0.1 convert_reduce_fusion.1
  15.5 12.1 %psum.35 = f32[64]{0:T(128)S(1)} all-reduce(f32[64]{0:T(128)S(1)} %get-tuple-element.7), channel_id=1, replica_groups=mesh['section'=4,'ctx'=4,'dp'=2] {'ctx'}, use_global_device_ids=true, to_apply=%region_6.0 | all-reduce | flops 64 | bytes 512 | tf_op jit(solution)/shard_map/psum | solution.py:102
  27.6 0.1 fusion.73
  27.8 0.0 copy-done.3
  27.8 0.2 fusion.39
  28.0 0.0 copy-start.9
  28.0 0.3 fusion.41
  28.3 1.2 convolution_bitcast_fusion
  29.5 0.0 all-reduce.3.cloned.1.call-update
  29.5 0.8 fusion.83
  30.3 0.0 copy-done.9
  30.3 0.1 convert_reduce_fusion
  30.5 0.6 broadcast_in_dim.11
  31.1 0.1 fusion.72
  31.2 9.5 %all-reduce = (f32[64]{0:T(128)S(1)}, f32[64]{0:T(128)S(1)}, f32[64]{0:T(128)S(1)}) all-reduce(f32[64]{0:T(128)S(1)} %get-tuple-element.5, f32[64]{0:T(128)S(1)} %fusion.72, f32[64]{0:T(128)S(1)} %convert_reduce_fusion), channel_id=1, replica_groups=mesh['section'=4,'ctx'=4,'dp'=2] {'ctx'}, use_global_device_ids=true, to_apply=%region_18.19 | all-reduce | flops 192 | bytes 1536 | tf_op jit(solution)/shard_map/psum | solution.py:102
  40.7 0.6 multiply_reduce_fusion.1
  41.3 0.6 multiply_reduce_fusion.2
  41.9 1.9 maximum_bitcast_fusion
  43.8 69.3 %all-gather.9.cloned.1.call-done = bf16[1,2048,1280]{2,1,0:T(8,128)(2,1)} async-done(((bf16[1,512,1280]{2,1,0:T(8,128)(2,1)}), bf16[1,2048,1280]{2,1,0:T(8,128)(2,1)}) %all-gather.9.cloned.1.call-update) | async-done | bytes 5242896 | tf_op jit(solution)/shard_map/all_gather | solution.py:109
  113.1 5.1 %fusion.6 = f32[256,1280]{1,0:T(8,128)} fusion(bf16[1,2048,1280]{2,1,0:T(8,128)(2,1)} %all-gather.9.cloned.1.call-done, bf16[128,2048]{1,0:T(8,128)(2,1)S(1)} %get-tuple-element.19, bf16[128,2048]{1,0:T(8,128)(2,1)S(1)} %get-tuple-element.18), kind=kOutput, calls=%fused_computation.6 | convolution fusion | flops 1344274432 | bytes 7602176 | tf_op jit(solution)/shard_map/dot_general | solution.py:113
  118.1 94.6 %all-gather.7.cloned.1.call-done = bf16[1,2048,1280]{2,1,0:T(8,128)(2,1)} async-done(((bf16[1,512,1280]{2,1,0:T(8,128)(2,1)}), bf16[1,2048,1280]{2,1,0:T(8,128)(2,1)}) %all-gather.7.cloned.1.call-update) | async-done | bytes 5242896 | tf_op jit(solution)/shard_map/all_gather | solution.py:108
  212.7 5.5 %fusion.85 = (f32[256,1280]{1,0:T(8,128)}, f32[256,1280]{1,0:T(8,128)}) fusion(bf16[1,2048,1280]{2,1,0:T(8,128)(2,1)} %all-gather.7.cloned.1.call-done, bf16[128,2048]{1,0:T(8,128)(2,1)S(1)} %get-tuple-element.19, bf16[128,2048]{1,0:T(8,128)(2,1)S(1)} %get-tuple-element.18), kind=kOutput, calls=%fused_computation.116 | convolution fusion | flops 1344602112 | bytes 8912896 | tf_op jit(solution)/shard_map/dot_general | solution.py:112
  218.2 92.7 %all-gather.11.cloned.1.call-done = bf16[1,1280,2048]{2,1,0:T(8,128)(2,1)} async-done(((bf16[1,1280,512]{2,1,0:T(8,128)(2,1)}), bf16[1,1280,2048]{2,1,0:T(8,128)(2,1)}) %all-gather.11.cloned.1.call-update) | async-done | bytes 5242896 | tf_op jit(solution)/shard_map/all_gather | solution.py:110
  310.9 4.1 %fusion.19 = bf16[128,2048]{1,0:T(8,128)(2,1)S(1)} fusion(bf16[1,1280,2048]{2,1,0:T(8,128)(2,1)} %all-gather.11.cloned.1.call-done, bf16[1,1,128,2048]{3,2,1,0:T(8,128)(2,1)S(1)} %copy-done.3, f32[256,1280]{1,0:T(8,128)} %fusion.6, f32[256,1280]{1,0:T(8,128)} %get-tuple-element.21, f32[256,1280]{1,0:T(8,128)} %get-tuple-element.20), kind=kOutput, calls=%fused_computation.16 | convolution fusion | flops 672694272 | bytes 8257536 | tf_op jit(solution)/shard_map/dot_general | solution.py:115
  315.1 0.0 copy-start.5
  315.1 1.5 collective-permute-start
  316.6 0.0 collective-permute-done.1
  316.6 0.0 copy-done.2
  316.6 0.0 slice-start
  316.6 1.8 fusion
  318.5 0.0 copy-done.5
  318.5 0.0 slice-start.1
  318.5 0.0 copy-start.4
  318.5 4.4 %fusion.4 = f32[128,2048]{1,0:T(8,128)S(1)} fusion(bf16[1,2048,1280]{2,1,0:T(8,128)(2,1)} %all-gather.9.cloned.1.call-done, f32[128,1280]{1,0:T(8,128)S(1)} %fusion, f32[256,1280]{1,0:T(8,128)S(1)} %copy-done.5), kind=kOutput, calls=%fused_computation.4 | convolution fusion | flops 672071680 | bytes 7602176 | tf_op jit(solution)/shard_map/tf,df->td/dot_general | solution.py:121
  322.9 0.0 slice-done
  322.9 0.0 slice-done.1
  322.9 0.0 copy-done.4
  323.0 1.8 fusion.12
  324.8 1.3 fusion.45
  326.1 1.2 fusion.57
  327.3 2.4 collective-permute-done
  329.7 0.8 copy.56
  330.5 1.9 copy.57
  (16 shorter events, 0.2 us)
Async XLA Ops:
  8.0 6.5 %copy-start = (f32[1,64,2048]{2,1,0:T(8,128)S(1)}, f32[1,64,2048]{2,1,0:T(8,128)}, u32[]{:S(2)}) copy-start(f32[1,64,2048]{2,1,0:T(8,128)} %param.18) | copy-start | bytes 1572868
  8.0 6.3 %copy-start.8 = (s32[1,1,128,6]{2,1,3,0:T(1,128)S(1)}, s32[1,1,128,6]{2,1,3,0:T(1,128)}, u32[]{:S(2)}) copy-start(s32[1,1,128,6]{2,1,3,0:T(1,128)} %param.15) | copy-start | bytes 9220
  8.0 6.3 %copy-start.1 = (bf16[1,1,128,2048]{3,2,1,0:T(8,128)(2,1)S(1)}, bf16[1,1,128,2048]{3,2,1,0:T(8,128)(2,1)}, u32[]{:S(2)}) copy-start(bf16[1,1,128,2048]{3,2,1,0:T(8,128)(2,1)} %param.12) | copy-start | bytes 1572868
  8.0 6.5 %copy-start.6 = (f32[1,2048]{1,0:T(1,128)S(1)}, f32[1,2048]{1,0:T(1,128)}, u32[]{:S(2)}) copy-start(f32[1,2048]{1,0:T(1,128)} %param.17) | copy-start | bytes 24580
  8.0 105.0 %all-gather.9.cloned.1.call-start = ((), (), s32[]{:S(2)}) async-start(), calls=%async_computation.2 | async-start | bytes 6553600 | tf_op jit(solution)/shard_map/all_gather | solution.py:109
  8.8 6.6 %copy-start.7 = (f32[1,1,128,6]{2,1,3,0:T(1,128)S(1)}, f32[1,1,128,6]{2,1,3,0:T(1,128)}, u32[]{:S(2)}) copy-start(f32[1,1,128,6]{2,1,3,0:T(1,128)} %param.16) | copy-start | bytes 9220
  8.8 19.0 %copy-start.3 = (bf16[1,1,128,2048]{3,2,1,0:T(8,128)(2,1)S(1)}, bf16[1,1,128,2048]{3,2,1,0:T(8,128)(2,1)}, u32[]{:S(2)}) copy-start(bf16[1,1,128,2048]{3,2,1,0:T(8,128)(2,1)} %param.11) | copy-start | bytes 1572868
  8.8 203.9 %all-gather.7.cloned.1.call-start = ((), (), s32[]{:S(2)}) async-start(), calls=%async_computation.1 | async-start | bytes 6553600 | tf_op jit(solution)/shard_map/all_gather | solution.py:108
  9.5 301.4 %all-gather.11.cloned.1.call-start = ((), (), s32[]{:S(2)}) async-start(), calls=%async_computation.3 | async-start | bytes 6553600 | tf_op jit(solution)/shard_map/all_gather | solution.py:110
  10.3 319.4 %all-reduce.3.cloned.1.call-start = ((), (), s32[]{:S(2)}) async-start(), calls=%async_computation | async-start | bytes 1048576 | tf_op jit(solution)/shard_map/psum | solution.py:134
  10.3 306.3 %collective-permute-start.1 = (bf16[128,2048]{1,0:T(8,128)(2,1)}, bf16[128,2048]{1,0:T(8,128)(2,1)S(1)}, u32[]{:S(2)}, u32[]{:S(2)}) collective-permute-start(bf16[128,2048]{1,0:T(8,128)(2,1)} %bitcast.11), channel_id=1, source_target_pairs={{8,0},{16,8},{24,16},{0,24},{9,1},{17,9},{25,17},{1,25},{10,2},{18... | collective-permute-start | bytes 1572872 | tf_op jit(solution)/shard_map/ppermute | solution.py:13
  28.0 2.3 copy-start.9
  310.9 5.7 %copy-start.2 = (bf16[1,1280,2048]{2,1,0:T(8,128)(2,1)S(1)}, bf16[1,1280,2048]{2,1,0:T(8,128)(2,1)}, u32[]{:S(2)}) copy-start(bf16[1,1280,2048]{2,1,0:T(8,128)(2,1)} %all-gather.11.cloned.1.call-done) | copy-start | bytes 15728644
  315.1 3.4 %copy-start.5 = (f32[256,1280]{1,0:T(8,128)S(1)}, f32[256,1280]{1,0:T(8,128)}, u32[]{:S(2)}) copy-start(f32[256,1280]{1,0:T(8,128)} %get-tuple-element.21) | copy-start | bytes 3932164
  315.1 14.6 %collective-permute-start = (bf16[128,2048]{1,0:T(8,128)(2,1)S(1)}, bf16[128,2048]{1,0:T(8,128)(2,1)S(1)}, u32[]{:S(2)}, u32[]{:S(2)}) collective-permute-start(bf16[128,2048]{1,0:T(8,128)(2,1)S(1)} %fusion.19), channel_id=1, source_target_pairs={{24,0},{0,8},{8,16},{16,24},{25,1},{1,9},{9,17},{17,25},{26,2},{2,... | collective-permute-start | bytes 1572872 | tf_op jit(solution)/shard_map/ppermute | solution.py:13
  316.6 6.3 %slice-start = ((s8[5242880]{0:T(1024)(128)(4,1)}), s8[4194304]{0:T(1024)(128)(4,1)S(1)}, s32[]{:S(2)}) async-start(s8[5242880]{0:T(1024)(128)(4,1)} %bitcast.128), calls=%async_computation.4 | async-start | bytes 8388608
  318.5 4.5 %slice-start.1 = ((s8[5242880]{0:T(1024)(128)(4,1)}), s8[1048576]{0:T(1024)(128)(4,1)S(1)}, s32[]{:S(2)}) async-start(s8[5242880]{0:T(1024)(128)(4,1)} %bitcast.128), calls=%async_computation.5 | async-start | bytes 2097152
  318.5 4.5 %copy-start.4 = (f32[256,1280]{1,0:T(8,128)S(1)}, f32[256,1280]{1,0:T(8,128)}, u32[]{:S(2)}) copy-start(f32[256,1280]{1,0:T(8,128)} %fusion.6) | copy-start | bytes 3932164
Sparse Core Ops, SparseCore 0:
  10.4 102.6 all-gather.8
  114.6 98.0 all-gather.6
  214.3 96.5 all-gather.10
Sparse Core Ops, SparseCore 1:
  29.6 196.5 all-reduce.2
where the time goes:
time: 340 us; the launch traced here: 339 us
  waiting for transfers between devices  261 us (77%)
  matrix products  26.9 us (8%)
  blocking collectives  21.6 us (6%)
  between operations  15.4 us (5%)
  starting transfers between devices  5.66 us (2%)
  other arithmetic  5.57 us (2%)
    all_gather x1, waiting for transfers between devices, shards(): lax.all_gather(gate_weight[0], 'ctx', axis=0, tiled=True)  94.6 us
    all_gather x1, waiting for transfers between devices, shards(): lax.all_gather(down_weight[0], 'ctx', axis=1, tiled=True)  92.7 us
    all_gather x1, waiting for transfers between devices, shards(): lax.all_gather(up_weight[0], 'ctx', axis=0, tiled=True)  69.3 us
    psum x2, blocking collectives, shards(): lax.psum((counts_a, counts_b, sums_a, sums_b), 'ctx')  21.6 us
  transfers between devices with their start and end apart: 6, of which 4 were waited for; matrix products, arithmetic and copies ran while one was open for 10% of the time, Pallas kernels for 0%

commit v1 on v0

--- a/solution.py
+++ b/solution.py
@@ -11,6 +11,25 @@
     devices = range(lax.axis_size(axis))
     route = [((i - distance) % len(devices), i) for i in devices]
     return lax.ppermute(block, axis, route)
+
+
+def siblings(axis):
+    size = lax.axis_size(axis)
+    return [(i, i ^ 1) for i in range(size)]
+
+
+def gather_split(block, axis, shard_axis):
+    if lax.axis_size("dp") % 2:
+        return lax.all_gather(block, axis, axis=shard_axis, tiled=True)
+    core = lax.axis_index("dp") % 2
+    rows = block.shape[0] // 2
+    mine = lax.dynamic_slice_in_dim(block, core * rows, rows, axis=0)
+    mine = lax.all_gather(mine, axis, axis=0, tiled=False)
+    other = lax.ppermute(mine, "dp", siblings("dp"))
+    both = jnp.stack([jnp.where(core == 0, mine, other), jnp.where(core == 0, other, mine)], axis=1)
+    if shard_axis == 0:
+        return both.reshape(-1, block.shape[1])
+    return both.reshape(-1, block.shape[0], block.shape[1]).transpose(1, 0, 2).reshape(block.shape[0], -1)
 
 
 def normalize(values_in, norm_gain):
@@ -105,9 +124,9 @@
     balance = jnp.stack([jnp.sum(frac_a * sums_a / length), jnp.sum(frac_b * sums_b / length)])
     stacked = jnp.concatenate([normed_a, normed_b], axis=0)
     gate_full, up_full, down_full = (
-        lax.all_gather(gate_weight[0], "ctx", axis=0, tiled=True),
-        lax.all_gather(up_weight[0], "ctx", axis=0, tiled=True),
-        lax.all_gather(down_weight[0], "ctx", axis=1, tiled=True),
+        gather_split(gate_weight[0], "ctx", 0),
+        gather_split(up_weight[0], "ctx", 0),
+        gather_split(down_weight[0], "ctx", 1),
     )
     gate_pre = jnp.dot(stacked, gate_full, preferred_element_type=jnp.float32)
     up_pre = jnp.dot(stacked, up_full, preferred_element_type=jnp.float32)

time: 340 us -> 236 us (0.69)
  waiting for transfers between devices: 261 us -> 140 us
  local copies, waits for them, and re-layouts: 3.31 us -> 19.4 us
  matrix products: 26.9 us -> 14.4 us
  other arithmetic: 5.57 us -> 18 us
    all_gather x3, waiting for transfers between devices: 257 us -> 132 us  [gather_split(): mine = lax.all_gather(mine, axis, axis=0, tiled=False)]
    another operation x0 -> x6, other arithmetic: none -> 11.8 us  [gather_split(): jnp.stack([jnp.where(core == 0, mine, other), jnp.where(core == 0, other,...]
    transpose x0 -> x1, local copies, waits for them, and re-layouts: none -> 7.89 us  [gather_split(): both.reshape(-1, block.shape[0], block.shape[1]).transpose(1, 0, 2)]
    ppermute x2, waiting for transfers between devices: 2.42 us -> 8.03 us  [shifted(): return lax.ppermute(block, axis, route)]
    dot_general x1, matrix products: 5.5 us -> 1.52 us  [shards(): gate_pre = jnp.dot(stacked, gate_full, preferred_element_type=jnp.float32)]
    unnamed x28 -> x38, local copies, waits for them, and re-layouts: 2.72 us -> 6.69 us
    dynamic_slice x0 -> x3, local copies, waits for them, and re-layouts: none -> 3.87 us  [gather_split(): mine = lax.dynamic_slice_in_dim(block, core * rows, rows, axis=0)]
  transfers between devices with their start and end apart: 6 -> 9, of which waited for: 4 -> 4; matrix products, arithmetic and copies ran while one was open for 10% -> 19% of each run, Pallas kernels for 0% -> 0%
where the time goes in v1:
time: 236 us; the launch traced here: 235 us
  waiting for transfers between devices  140 us (59%)
  blocking collectives  21.9 us (9%)
  local copies, waits for them, and re-layouts  19.4 us (8%)
  other arithmetic  18 us (8%)
  between operations  15.5 us (7%)
  matrix products  14.4 us (6%)
  starting transfers between devices  5.86 us (2%)
    all_gather x3, waiting for transfers between devices, gather_split(): mine = lax.all_gather(mine, axis, axis=0, tiled=False)  132 us
    psum x2, blocking collectives, shards(): lax.psum((counts_a, counts_b, sums_a, sums_b), 'ctx')  21.9 us
    another operation x6, other arithmetic, gather_split(): jnp.stack([jnp.where(core == 0, mine, other), jnp.where(core == 0, other,...  11.8 us
    ppermute x2, waiting for transfers between devices, shifted(): return lax.ppermute(block, axis, route)  8.03 us
    transpose x1, local copies, waits for them, and re-layouts, gather_split(): both.reshape(-1, block.shape[0], block.shape[1]).transpose(1, 0, 2)  7.89 us
    unnamed x38, local copies, waits for them, and re-layouts  6.69 us
    ppermute x2, starting transfers between devices, shifted(): return lax.ppermute(block, axis, route)  5.69 us
  transfers between devices with their start and end apart: 9, of which 4 were waited for; matrix products, arithmetic and copies ran while one was open for 19% of the time, Pallas kernels for 0%

profile of v1, /device:TPU:0, one launch (start us, length us, event | category | flops | bytes accessed | tf_op | source)
XLA Modules:
  0.0 235.5 jit_solution(3038158463023170178)
XLA Ops:
  8.0 0.0 copy-start
  8.0 0.0 all-gather.8.cloned.1.call-start
  8.1 1.2 copy-done
  9.3 0.9 constant_dynamic-slice_fusion
  10.2 0.0 all-gather.8.cloned.1.call-update
  10.2 0.0 all-gather.6.cloned.1.call-start
  10.3 0.0 copy-start.12
  10.3 0.0 copy-start.4
  10.3 2.1 constant_dynamic-slice_fusion.1
  12.4 0.0 all-gather.6.cloned.1.call-update
  12.4 0.0 all-gather.4.cloned.1.call-start
  12.5 0.9 constant_dynamic-slice_fusion.2
  13.4 0.0 all-gather.4.cloned.1.call-update
  13.4 0.0 all-reduce.3.cloned.1.call-start
  13.5 4.0 %collective-permute-start.4 = (bf16[128,2048]{1,0:T(8,128)(2,1)}, bf16[128,2048]{1,0:T(8,128)(2,1)S(1)}, u32[]{:S(2)}, u32[]{:S(2)}) collective-permute-start(bf16[128,2048]{1,0:T(8,128)(2,1)} %bitcast.150), channel_id=1, source_target_pairs={{8,0},{16,8},{24,16},{0,24},{9,1},{17,9},{25,17},{1,25},{10,2},{18... | collective-permute-start | bytes 1572872 | tf_op jit(solution)/shard_map/ppermute | solution.py:13
  17.5 0.2 fusion.25
  17.7 0.8 fusion.69
  18.5 0.1 convert_reduce_fusion.1
  18.7 12.5 %psum.35 = f32[64]{0:T(128)S(1)} all-reduce(f32[64]{0:T(128)S(1)} %get-tuple-element.7), channel_id=1, replica_groups=mesh['section'=4,'ctx'=4,'dp'=2] {'ctx'}, use_global_device_ids=true, to_apply=%region_6.0 | all-reduce | flops 64 | bytes 512 | tf_op jit(solution)/shard_map/psum | solution.py:121
  31.2 36.9 %all-gather.8.cloned.1.call-done = bf16[4,640,512]{2,1,0:T(8,128)(2,1)} async-done(((bf16[1,640,512]{2,1,0:T(8,128)(2,1)}), bf16[4,640,512]{2,1,0:T(8,128)(2,1)}) %all-gather.8.cloned.1.call-update) | async-done | bytes 2621456 | tf_op jit(solution)/shard_map/all_gather | solution.py:27
  68.1 0.2 fusion.20
  68.3 0.8 fusion.68
  69.1 54.0 %all-gather.6.cloned.1.call-done = bf16[4,256,1280]{2,1,0:T(8,128)(2,1)} async-done(((bf16[1,256,1280]{2,1,0:T(8,128)(2,1)}), bf16[4,256,1280]{2,1,0:T(8,128)(2,1)}) %all-gather.6.cloned.1.call-update) | async-done | bytes 2621456 | tf_op jit(solution)/shard_map/all_gather | solution.py:27
  123.1 0.0 collective-permute-start.1
  123.1 0.1 fusion.58
  123.2 1.0 fusion.22
  124.2 0.8 copy-done.6
  125.0 1.2 convolution_bitcast_fusion.1
  126.2 0.0 all-reduce.3.cloned.1.call-update
  126.4 0.6 broadcast_in_dim.11
  126.9 0.1 convert_reduce_fusion
  127.1 9.4 %all-reduce = (f32[64]{0:T(128)S(1)}, f32[64]{0:T(128)S(1)}, f32[64]{0:T(128)S(1)}) all-reduce(f32[64]{0:T(128)S(1)} %get-tuple-element.5, f32[64]{0:T(128)S(1)} %get-tuple-element.32, f32[64]{0:T(128)S(1)} %convert_reduce_fusion), channel_id=1, replica_groups=mesh['section'=4,'ctx'=4,'dp'=2] {'ctx'}, use_global_device_ids=true, to_apply=%region_18.19 | all-reduce | flops 192 | bytes 1536 | tf_op jit(solution)/shard_map/psum | solution.py:121
  136.4 0.7 multiply_reduce_fusion.1
  137.1 0.6 multiply_reduce_fusion.2
  137.7 1.1 fusion.41
  138.8 41.4 %all-gather.4.cloned.1.call-done = bf16[4,256,1280]{2,1,0:T(8,128)(2,1)} async-done(((bf16[1,256,1280]{2,1,0:T(8,128)(2,1)}), bf16[4,256,1280]{2,1,0:T(8,128)(2,1)}) %all-gather.4.cloned.1.call-update) | async-done | bytes 2621456 | tf_op jit(solution)/shard_map/all_gather | solution.py:27
  180.2 0.0 collective-permute-start
  180.2 1.8 maximum_bitcast_fusion
  182.1 2.9 %select_bitcast_fusion.1 = (bf16[4,1,640,512]{3,2,1,0:T(8,128)(2,1)S(1)}, bf16[4,1,640,512]{3,2,1,0:T(8,128)(2,1)S(1)}) fusion(bf16[4,640,512]{2,1,0:T(8,128)(2,1)} %all-gather.8.cloned.1.call-done, bf16[4,640,512]{2,1,0:T(8,128)(2,1)} %collective-permute-done.2, pred[]{:T(512)S(6)} %eq.42), kind=kLoop, calls=%fused_computation.4 | loop fusion | flops 2621440 | bytes 10485761 | tf_op jit(solution)/shard_map/stack | solution.py:29
  185.0 2.8 %pad_maximum_fusion.2 = bf16[4,2,640,512]{3,2,1,0:T(8,128)(2,1)} fusion(bf16[4,1,640,512]{3,2,1,0:T(8,128)(2,1)S(1)} %get-tuple-element.23, bf16[4,1,640,512]{3,2,1,0:T(8,128)(2,1)S(1)} %get-tuple-element.22), kind=kLoop, calls=%fused_computation.2 | loop fusion | flops 2621440 | bytes 10485760 | tf_op jit(solution)/shard_map/stack | solution.py:29
  187.8 7.9 %copy.36 = bf16[1280,4,512]{0,2,1:T(8,128)(2,1)} copy(bf16[1280,4,512]{2,0,1:T(8,128)(2,1)} %bitcast.139) | data formatting | bytes 10485760 | tf_op jit(solution)/shard_map/transpose | solution.py:32
  195.7 0.0 collective-permute-done.1
  195.7 2.9 %select_bitcast_fusion.3 = (bf16[4,1,256,1280]{3,2,0,1:T(8,128)(2,1)S(1)}, bf16[4,1,256,1280]{3,2,0,1:T(8,128)(2,1)S(1)}) fusion(bf16[4,256,1280]{2,1,0:T(8,128)(2,1)} %all-gather.6.cloned.1.call-done, bf16[4,256,1280]{2,1,0:T(8,128)(2,1)} %collective-permute-done.1, pred[]{:T(512)S(6)} %eq.42), kind=kLoop, calls=%fused_computation.6 | loop fusion | flops 2621440 | bytes 10485761 | tf_op jit(solution)/shard_map/stack | solution.py:29
  198.6 0.5 pad_maximum_fusion.1
  199.0 0.0 copy-start.7
  199.1 0.0 copy-start.8
  199.1 0.3 copy.34
  199.4 0.7 copy-done.7
  200.1 0.2 copy-done.8
  200.3 2.6 %fusion.29 = f32[256,1280]{1,0:T(8,128)} fusion(bf16[2048,1280]{1,0:T(8,128)(2,1)S(1)} %bitcast.140, bf16[128,2048]{1,0:T(8,128)(2,1)S(1)} %copy-done.7, bf16[128,2048]{1,0:T(8,128)(2,1)S(1)} %copy-done.8), kind=kOutput, calls=%fused_computation.49 | convolution fusion | flops 1344274432 | bytes 7602176 | tf_op jit(solution)/shard_map/dot_general | solution.py:132
  202.9 0.0 collective-permute-done
  202.9 2.2 select_bitcast_fusion.5
  205.1 0.5 pad_maximum_fusion
  205.6 1.5 fusion.70
  207.2 1.8 fusion.2
  209.0 1.7 collective-permute-start.3
  210.8 0.9 convolution_bitcast_fusion
  211.6 1.8 fusion.49
  213.4 0.0 copy-start.1
  213.4 2.0 fusion.26
  215.4 1.2 fusion.40
  216.6 8.0 %collective-permute-done.3 = bf16[128,2048]{1,0:T(8,128)(2,1)} collective-permute-done((bf16[128,2048]{1,0:T(8,128)(2,1)S(1)}, bf16[128,2048]{1,0:T(8,128)(2,1)}, u32[]{:S(2)}, u32[]{:S(2)}) %collective-permute-start.3) | collective-permute-done | bytes 524320 | tf_op jit(solution)/shard_map/ppermute | solution.py:13
  224.6 1.9 copy.77
  226.5 1.9 copy.78
  (42 shorter events, 0.2 us)
Async XLA Ops:
  8.0 1.3 copy-start
  8.0 4.5 %copy-start.10 = (bf16[1,512,1280]{2,1,0:T(8,128)(2,1)S(1)}, bf16[1,512,1280]{2,1,0:T(8,128)(2,1)}, u32[]{:S(2)}) copy-start(bf16[1,512,1280]{2,1,0:T(8,128)(2,1)} %param.19) | copy-start | bytes 3932164
  8.0 60.1 %all-gather.8.cloned.1.call-start = ((), (), s32[]{:S(2)}) async-start(), calls=%async_computation.2 | async-start | bytes 3276800 | tf_op jit(solution)/shard_map/all_gather | solution.py:27
  10.2 7.2 %copy-start.13 = (s32[1,1,128,6]{2,1,3,0:T(1,128)S(1)}, s32[1,1,128,6]{2,1,3,0:T(1,128)}, u32[]{:S(2)}) copy-start(s32[1,1,128,6]{2,1,3,0:T(1,128)} %param.15) | copy-start | bytes 9220
  10.2 7.2 %copy-start.2 = (bf16[1,1,128,2048]{3,2,1,0:T(8,128)(2,1)S(1)}, bf16[1,1,128,2048]{3,2,1,0:T(8,128)(2,1)}, u32[]{:S(2)}) copy-start(bf16[1,1,128,2048]{3,2,1,0:T(8,128)(2,1)} %param.12) | copy-start | bytes 1572868
  10.2 7.4 %copy-start.3 = (f32[1,64,2048]{2,1,0:T(8,128)S(1)}, f32[1,64,2048]{2,1,0:T(8,128)}, u32[]{:S(2)}) copy-start(f32[1,64,2048]{2,1,0:T(8,128)} %param.18) | copy-start | bytes 1572868
  10.2 7.4 %copy-start.11 = (f32[1,2048]{1,0:T(1,128)S(1)}, f32[1,2048]{1,0:T(1,128)}, u32[]{:S(2)}) copy-start(f32[1,2048]{1,0:T(1,128)} %param.17) | copy-start | bytes 24580
  10.2 112.8 %all-gather.6.cloned.1.call-start = ((), (), s32[]{:S(2)}) async-start(), calls=%async_computation.1 | async-start | bytes 3276800 | tf_op jit(solution)/shard_map/all_gather | solution.py:27
  10.3 8.2 %copy-start.12 = (f32[1,1,128,6]{2,1,3,0:T(1,128)S(1)}, f32[1,1,128,6]{2,1,3,0:T(1,128)}, u32[]{:S(2)}) copy-start(f32[1,1,128,6]{2,1,3,0:T(1,128)} %param.16) | copy-start | bytes 9220
  10.3 57.8 %copy-start.4 = (bf16[1,1,128,2048]{3,2,1,0:T(8,128)(2,1)S(1)}, bf16[1,1,128,2048]{3,2,1,0:T(8,128)(2,1)}, u32[]{:S(2)}) copy-start(bf16[1,1,128,2048]{3,2,1,0:T(8,128)(2,1)} %param.11) | copy-start | bytes 1572868
  12.4 167.8 %all-gather.4.cloned.1.call-start = ((), (), s32[]{:S(2)}) async-start(), calls=%async_computation | async-start | bytes 3276800 | tf_op jit(solution)/shard_map/all_gather | solution.py:27
  13.4 211.2 %all-reduce.3.cloned.1.call-start = ((), (), s32[]{:S(2)}) async-start(), calls=%async_computation.3 | async-start | bytes 1048576 | tf_op jit(solution)/shard_map/psum | solution.py:153
  13.5 197.3 %collective-permute-start.4 = (bf16[128,2048]{1,0:T(8,128)(2,1)}, bf16[128,2048]{1,0:T(8,128)(2,1)S(1)}, u32[]{:S(2)}, u32[]{:S(2)}) collective-permute-start(bf16[128,2048]{1,0:T(8,128)(2,1)} %bitcast.150), channel_id=1, source_target_pairs={{8,0},{16,8},{24,16},{0,24},{9,1},{17,9},{25,17},{1,25},{10,2},{18... | collective-permute-start | bytes 1572872 | tf_op jit(solution)/shard_map/ppermute | solution.py:13
  31.2 95.1 %copy-start.14 = (s32[1,1,128,6]{2,1,3,0:T(1,128)S(1)}, s32[1,1,128,6]{2,1,3,0:T(1,128)}, u32[]{:S(2)}) copy-start(s32[1,1,128,6]{2,1,3,0:T(1,128)} %param.14) | copy-start | bytes 9220
  68.1 114.0 %collective-permute-start.2 = (bf16[4,640,512]{2,1,0:T(8,128)(2,1)}, bf16[4,640,512]{2,1,0:T(8,128)(2,1)}, u32[]{:S(2)}, u32[]{:S(2)}) collective-permute-start(bf16[4,640,512]{2,1,0:T(8,128)(2,1)} %all-gather.8.cloned.1.call-done), channel_id=1, source_target_pairs={{0,1},{1,0},{2,3},{3,2},{4,5},{5,4},{6,7},{7,6},{8,9},{9,8},{10,11... | collective-permute-start | bytes 7864328 | tf_op jit(solution)/shard_map/ppermute | solution.py:28
  123.1 72.6 %collective-permute-start.1 = (bf16[4,256,1280]{2,1,0:T(8,128)(2,1)}, bf16[4,256,1280]{2,1,0:T(8,128)(2,1)}, u32[]{:S(2)}, u32[]{:S(2)}) collective-permute-start(bf16[4,256,1280]{2,1,0:T(8,128)(2,1)} %all-gather.6.cloned.1.call-done), channel_id=1, source_target_pairs={{0,1},{1,0},{2,3},{3,2},{4,5},{5,4},{6,7},{7,6},{8,9},{9,8},{10,11... | collective-permute-start | bytes 7864328 | tf_op jit(solution)/shard_map/ppermute | solution.py:28
  124.2 0.8 copy-start.6
  180.2 22.7 %collective-permute-start = (bf16[4,256,1280]{2,1,0:T(8,128)(2,1)}, bf16[4,256,1280]{2,1,0:T(8,128)(2,1)}, u32[]{:S(2)}, u32[]{:S(2)}) collective-permute-start(bf16[4,256,1280]{2,1,0:T(8,128)(2,1)} %all-gather.4.cloned.1.call-done), channel_id=1, source_target_pairs={{0,1},{1,0},{2,3},{3,2},{4,5},{5,4},{6,7},{7,6},{8,9},{9,8},{10,11... | collective-permute-start | bytes 7864328 | tf_op jit(solution)/shard_map/ppermute | solution.py:28
  199.0 1.0 copy-start.7
  199.1 1.2 copy-start.8
  200.3 2.6 %copy-start.5 = (bf16[4,256,1280]{2,1,0:T(8,128)(2,1)S(1)}, bf16[4,256,1280]{2,1,0:T(8,128)(2,1)}, u32[]{:S(2)}) copy-start(bf16[4,256,1280]{2,1,0:T(8,128)(2,1)} %all-gather.4.cloned.1.call-done) | copy-start | bytes 7864324
  202.9 4.3 %slice-start = ((s8[5242880]{0:T(1024)(128)(4,1)}), s8[4194304]{0:T(1024)(128)(4,1)S(1)}, s32[]{:S(2)}) async-start(s8[5242880]{0:T(1024)(128)(4,1)} %bitcast.133), calls=%async_computation.4 | async-start | bytes 8388608
  205.1 2.0 slice-start.1
  205.6 1.6 copy-start.9
  209.0 15.6 %collective-permute-start.3 = (bf16[128,2048]{1,0:T(8,128)(2,1)S(1)}, bf16[128,2048]{1,0:T(8,128)(2,1)}, u32[]{:S(2)}, u32[]{:S(2)}) collective-permute-start(bf16[128,2048]{1,0:T(8,128)(2,1)S(1)} %fusion.2), channel_id=1, source_target_pairs={{24,0},{0,8},{8,16},{16,24},{25,1},{1,9},{9,17},{17,25},{26,2},{2,... | collective-permute-start | bytes 1572872 | tf_op jit(solution)/shard_map/ppermute | solution.py:13
  213.4 14.9 %copy-start.1 = (bf16[1,1280,512]{2,1,0:T(8,128)(2,1)S(1)}, bf16[1,1280,512]{2,1,0:T(8,128)(2,1)}, u32[]{:S(2)}) copy-start(bf16[1,1280,512]{2,1,0:T(8,128)(2,1)} %param.21) | copy-start | bytes 3932164
Sparse Core Ops, SparseCore 0:
  10.4 57.6 all-gather.7
  69.7 53.3 all-gather.5
  124.7 55.5 all-gather.3
Sparse Core Ops, SparseCore 1:
  126.3 92.1 all-reduce.2
